TPU v7x, 256 devices: a whole 4x4x8 slice. The times are simulated.
256 devices in a mesh: img: 16 (over y, x), row: 16 (over z, core).
Axes of the slice: x: 4, y: 4, z: 8, core: 2. Of those that a mesh axis runs over, the one named last changes fastest.
Arguments:
- latent: bfloat16 [1024, 128, 512], P(('img', 'row')), parts along dimension 0, may hold values from -8 to 8
- attn_gain: float32 [512], replicated, may hold values from 0.5 to 1.5
- attn_shift: float32 [512], replicated, may hold values from -3 to 3
- w_query: bfloat16 [512, 512], replicated, may hold values from -2 to 2
- w_key: bfloat16 [512, 512], replicated, may hold values from -2 to 2
- w_value: bfloat16 [512, 512], replicated, may hold values from -0.25 to 0.25
- w_out: bfloat16 [512, 512], replicated, may hold values from -0.25 to 0.25
- conv_gain: float32 [512], replicated, may hold values from 0.5 to 1.5
- conv_shift: float32 [512], replicated, may hold values from -3 to 3
- w_conv: bfloat16 [3, 3, 512, 512], replicated, may hold values from -0.09375 to 0.09375
- conv_bias: float32 [512], replicated, may hold values from -3 to 3
Outputs:
- encoded: bfloat16 [1024, 128, 512], P(('img', 'row')), parts along dimension 0
There are 16 independent parts, one for each index of `img`. A program takes and returns all parts, laid end to end along the dimension named above; an argument that names none is the same for every part. Nothing has to cross between parts.
All inputs are finite; a program needn't handle non-finite values.
Results may differ from a plain program's by a relative error of at most 0.011.
Values may be sent and summed in bfloat16 or wider, within the bound.
No kernel may reach another device: no remote copies, remote signals or barrier semaphores. Data moves between devices by JAX's collectives and lax.ppermute only.
A program may use at most 128 MiB of HBM per device.

v0:
```python
import jax
import jax.numpy as jnp
from jax import lax
from jax.sharding import PartitionSpec as P

C = 512
GROUPS = 32
W = 128
epsilon = 1e-06


def copy_for_each(shard, axis):
    copies = jnp.broadcast_to(shard, (lax.axis_size(axis), *shard.shape))
    return lax.all_to_all(copies, axis, split_axis=0, concat_axis=0, tiled=True)


def taken_together(shard, axis):
    return copy_for_each(shard, axis).sum(axis=0)


def together(arrays, axis):
    line, at, done = (jnp.concatenate([a.reshape(-1) for a in arrays]), 0, [])
    total = taken_together(line, axis)
    for a in arrays:
        done.append(total[at : at + a.size].reshape(a.shape))
        at += a.size
    return tuple(done)


def with_halo(cells, sides, width):
    for axis, dim in sides:
        count = lax.axis_size(axis)
        ends = count - 1
        head = lax.slice_in_dim(cells, 0, width, axis=dim)
        tail = lax.slice_in_dim(cells, cells.shape[dim] - width, cells.shape[dim], axis=dim)
        cells = jnp.concatenate(
            [
                lax.ppermute(tail, axis, [(i, (i + 1) % count) for i in range(ends)]),
                cells,
                lax.ppermute(head, axis, [((i + 1) % count, i) for i in range(ends)]),
            ],
            axis=dim,
        )
    return cells


def group_stats(grouped, count):
    first, second = together(
        (jnp.sum(grouped, axis=(0, 2)), jnp.sum(grouped * grouped, axis=(0, 2))), "row"
    )
    centre = first / count
    spread = second / count - centre * centre
    return (centre, spread)


def group_norm(field, gain, shift):
    grouped = field.reshape(field.shape[0], GROUPS, C // GROUPS)
    count = field.shape[0] * lax.axis_size("row") * (C // GROUPS)
    centre, spread = group_stats(grouped, count)
    normed = (grouped - centre[None, :, None]) * lax.rsqrt(spread + epsilon)[None, :, None]
    return normed.reshape(field.shape) * gain + shift


def attend(carry, key_piece, value_piece, queries):
    maxima, denominator, accumulated = carry
    scaling = 1.0 / jnp.sqrt(jnp.float32(C))
    scores = (
        jnp.einsum("qc,kc->qk", queries, key_piece, preferred_element_type=jnp.float32) * scaling
    )
    newest = jnp.maximum(maxima, jnp.max(scores, axis=1))
    expo = jnp.exp(scores - newest[:, None])
    denominator = jnp.sum(expo, axis=1)
    accumulated = jnp.dot(
        expo.astype(jnp.bfloat16), value_piece, preferred_element_type=jnp.float32
    )
    return (newest, denominator, accumulated)


def local(
    latent,
    attn_gain,
    attn_shift,
    w_query,
    w_key,
    w_value,
    w_out,
    conv_gain,
    conv_shift,
    w_conv,
    conv_bias,
):
    local_rows = latent.shape[0]
    positions = latent.reshape(local_rows * W, C)
    normed = group_norm(positions.astype(jnp.float32), attn_gain, attn_shift).astype(jnp.bfloat16)
    queries = jnp.dot(normed, w_query, preferred_element_type=jnp.float32).astype(jnp.bfloat16)
    count_rows = positions.shape[0]
    start_carry = (
        jnp.full((count_rows,), -1e30, jnp.float32),
        jnp.zeros((count_rows,), jnp.float32),
        jnp.zeros((count_rows, C), jnp.float32),
    )
    piece = lax.all_gather(normed, "row", axis=0, tiled=True)
    key_piece = jnp.dot(piece, w_key, preferred_element_type=jnp.float32).astype(jnp.bfloat16)
    value_piece = jnp.dot(piece, w_value, preferred_element_type=jnp.float32).astype(jnp.bfloat16)
    maxima, denominator, accumulated = attend(start_carry, key_piece, value_piece, queries)
    attended = (accumulated / denominator[:, None]).astype(jnp.bfloat16)
    hidden = (
        positions.astype(jnp.float32) + jnp.dot(attended, w_out, preferred_element_type=jnp.float32)
    ).astype(jnp.bfloat16)
    activated = jax.nn.silu(group_norm(hidden.astype(jnp.float32), conv_gain, conv_shift)).astype(
        jnp.bfloat16
    )
    activated = activated.reshape(local_rows, W, C)
    bordered = with_halo(activated, (("row", 0),), 1)
    padded = jnp.pad(bordered, ((0, 0), (1, 1), (0, 0)))
    convolved = jnp.zeros((local_rows * W, C), jnp.float32)
    for row_tap in range(3):
        for col_tap in range(3):
            window = padded[row_tap : row_tap + local_rows, col_tap : col_tap + W].reshape(
                local_rows * W, C
            )
            convolved = convolved + jnp.dot(
                window, w_conv[row_tap, col_tap], preferred_element_type=jnp.float32
            )
    encoded = hidden.astype(jnp.float32) + (convolved + conv_bias)
    return encoded.astype(jnp.bfloat16).reshape(local_rows, W, C)


def solution(mesh):
    in_specs = (P(("img", "row"), None, None), P(), P(), P(), P(), P(), P(), P(), P(), P(), P())
    out_specs = P(("img", "row"), None, None)
    return jax.shard_map(local, mesh=mesh, in_specs=in_specs, out_specs=out_specs, check_vma=False)
```

profile of v0, /device:TPU:1, one launch (start us, length us, event | category | flops | bytes accessed | tf_op | source)
XLA Modules:
  0.0 157.1 jit_solution(7887998248014053439)
XLA Ops:
  6.5 1.3 convert_reduce_fusion.1
  7.8 0.1 reduce_sum.74
  7.9 0.1 reduce_sum.80
  8.0 0.1 reduce_sum.75
  8.1 0.1 reduce_sum.96
  8.2 0.1 pad_maximum_fusion.2
  8.3 16.8 %all_to_all.12 = f32[16,1,64]{2,1,0:T(1,128)S(1)} all-to-all(f32[16,1,64]{2,1,0:T(1,128)S(1)} %broadcast_in_dim.6), channel_id=1, replica_groups=mesh['img'=16,'row'=16] {'row'}, dimensions={0} | all-to-all | bytes 8192 | tf_op jit(solution)/shard_map/all_to_all | solution.py:14
  25.1 0.1 slice_multiply_fusion.1
  25.2 0.1 sub.40
  25.3 0.1 sub.41
  25.4 0.1 mul.68
  25.4 0.1 mul.69
  25.5 2.1 %fusion.31 = bf16[512,512]{1,0:T(8,128)(2,1)} fusion(bf16[4,128,512]{2,1,0:T(8,128)(2,1)} %param.11, f32[512]{0:T(512)} %param.13, f32[512]{0:T(512)} %param.12, f32[512]{0:T(512)S(1)} %mul.69, f32[512]{0:T(512)S(1)} %sub.41), kind=kLoop, calls=%fused_computation.46 | loop fusion | flops 1572864 | bytes 1056768 | tf_op jit(solution)/shard_map/convert_element_type | solution.py:94
  27.6 0.0 all-gather.2.cloned.1.call-update
  27.6 1.6 %convolution_convert_fusion.2 = bf16[512,512]{1,0:T(8,128)(2,1)S(1)} fusion(bf16[512,512]{1,0:T(8,128)(2,1)} %fusion.31, bf16[512,512]{1,0:T(8,128)(2,1)} %param.14), kind=kOutput, calls=%fused_computation.28 | convolution fusion | flops 268697600 | bytes 1572864 | tf_op jit(solution)/shard_map/dot_general | solution.py:95
  29.2 51.1 %all-gather.2.cloned.1.call-done = bf16[8192,512]{1,0:T(8,128)(2,1)} async-done(((bf16[512,512]{1,0:T(8,128)(2,1)}), bf16[8192,512]{1,0:T(8,128)(2,1)}) %all-gather.2.cloned.1.call-update) | async-done | bytes 8388624 | tf_op jit(solution)/shard_map/all_gather | solution.py:102
  80.4 14.5 %multiply_reduce_fusion = (f32[512]{0:T(512)S(1)}, f32[512,8192]{1,0:T(8,128)}) fusion(bf16[512,512]{1,0:T(8,128)(2,1)S(1)} %convolution_convert_fusion.2, bf16[8192,512]{1,0:T(8,128)(2,1)} %all-gather.2.cloned.1.call-done, bf16[512,512]{1,0:T(8,128)(2,1)S(1)} %copy-done), kind=kOutput, calls=%fused_computation.1 | convolution fusion | flops 8602517504 | bytes 26216448 | tf_op jit(solution)/shard_map/qc,kc->qk/dot_general | solution.py:68
  94.9 8.7 %fusion = f32[512]{0:T(512)S(1)} fusion(f32[512,8192]{1,0:T(8,128)} %get-tuple-element.24, f32[512]{0:T(512)S(1)} %broadcast_maximum_fusion), kind=kLoop, calls=%fused_computation.2 | loop fusion | flops 12582400 | bytes 16781312 | tf_op jit(solution)/shard_map/reduce_sum | solution.py:72
  103.6 17.2 %fusion.15 = bf16[512,512]{1,0:T(8,128)(2,1)S(1)} fusion(bf16[8192,512]{1,0:T(8,128)(2,1)} %all-gather.2.cloned.1.call-done, bf16[512,512]{1,0:T(8,128)(2,1)S(1)} %copy-done.5, f32[512,8192]{1,0:T(8,128)} %get-tuple-element.24, f32[512]{0:T(512)S(1)} %broadcast_maximum_fusion, f32[512]{0:T(512)S(1)} %fusion), kind=kOutput, calls=%fused_computation.31 | convolution fusion | flops 8607236096 | bytes 26218496 | tf_op jit(solution)/shard_map/dot_general | solution.py:73
  120.8 0.5 convert_reduce_fusion
  121.3 0.1 reduce_sum.100
  121.4 0.3 reduce_sum.101
  121.7 0.1 reduce_sum.103
  121.8 0.1 reduce_sum.104
  121.9 0.1 pad_maximum_fusion.3
  122.0 11.4 %all_to_all.13 = f32[16,1,64]{2,1,0:T(1,128)S(1)} all-to-all(f32[16,1,64]{2,1,0:T(1,128)S(1)} %broadcast_in_dim.8), channel_id=1, replica_groups=mesh['img'=16,'row'=16] {'row'}, dimensions={0} | all-to-all | bytes 8192 | tf_op jit(solution)/shard_map/all_to_all | solution.py:14
  133.4 0.1 slice_multiply_fusion
  133.5 0.1 sub.47
  133.6 0.1 sub.48
  133.7 0.1 mul.78
  133.7 0.1 mul.79
  133.8 0.4 fusion.27
  134.2 2.7 %collective-permute-start = (bf16[1,128,512]{2,1,0:T(8,128)(2,1)S(1)}, bf16[1,128,512]{2,1,0:T(8,128)(2,1)S(1)}, u32[]{:S(2)}, u32[]{:S(2)}) collective-permute-start(bf16[1,128,512]{2,1,0:T(8,128)(2,1)S(1)} %get-tuple-element.17), channel_id=1, source_target_pairs={{0,1},{1,2},{2,3},{3,4},{4,5},{5,6},{6,7},{7,8},{8,9},{9,10},{10,1... | collective-permute-start | bytes 393224 | tf_op jit(solution)/shard_map/ppermute | solution.py:38
  137.0 1.9 %collective-permute-start.1 = (bf16[1,128,512]{2,1,0:T(8,128)(2,1)S(1)}, bf16[1,128,512]{2,1,0:T(8,128)(2,1)S(1)}, u32[]{:S(2)}, u32[]{:S(2)}) collective-permute-start(bf16[1,128,512]{2,1,0:T(8,128)(2,1)S(1)} %get-tuple-element.18), channel_id=1, source_target_pairs={{1,0},{2,1},{3,2},{4,3},{5,4},{6,5},{7,6},{8,7},{9,8},{10,9},{11,1... | collective-permute-start | bytes 393224 | tf_op jit(solution)/shard_map/ppermute | solution.py:40
  138.9 4.3 %collective-permute-done.1 = bf16[1,128,512]{2,1,0:T(8,128)(2,1)S(1)} collective-permute-done((bf16[1,128,512]{2,1,0:T(8,128)(2,1)S(1)}, bf16[1,128,512]{2,1,0:T(8,128)(2,1)S(1)}, u32[]{:S(2)}, u32[]{:S(2)}) %collective-permute-start.1) | collective-permute-done | bytes 131104 | tf_op jit(solution)/shard_map/ppermute | solution.py:40
  143.3 0.2 fusion.36
  143.5 0.4 fusion.58
  143.9 1.7 %fusion.46 = f32[512,512]{1,0:T(8,128)S(1)} fusion(bf16[512,512]{1,0:T(8,128)(2,1)S(1)} %bitcast.82, bf16[3,3,512,512]{3,2,1,0:T(8,128)(2,1)} %param.20), kind=kOutput, calls=%fused_computation.65 | convolution fusion | flops 268435456 | bytes 2097152 | tf_op jit(solution)/shard_map/dot_general | solution.py:122
  145.6 0.1 pad_maximum_fusion
  145.7 0.1 slice-done.1
  145.8 0.4 convolution_add_fusion.6
  146.3 0.4 convolution_add_fusion.5
  146.7 0.4 convolution_add_fusion.4
  147.2 0.4 convolution_add_fusion.3
  147.6 0.4 fusion.37
  148.1 0.4 convolution_add_fusion.2
  148.5 0.4 convolution_add_fusion.1
  149.0 1.3 fusion.10
  (26 shorter events, 0.1 us)
Async XLA Ops:
  6.5 73.8 %copy-start = (bf16[512,512]{1,0:T(8,128)(2,1)S(1)}, bf16[512,512]{1,0:T(8,128)(2,1)}, u32[]{:S(2)}) copy-start(bf16[512,512]{1,0:T(8,128)(2,1)} %param.15) | copy-start | bytes 1572868
  6.5 73.8 %all-gather.2.cloned.1.call-start = ((), (), s32[]{:S(2)}) async-start(), calls=%async_computation.2 | async-start | bytes 8912896 | tf_op jit(solution)/shard_map/all_gather | solution.py:102
  94.9 8.7 %copy-start.5 = (bf16[512,512]{1,0:T(8,128)(2,1)S(1)}, bf16[512,512]{1,0:T(8,128)(2,1)}, u32[]{:S(2)}) copy-start(bf16[512,512]{1,0:T(8,128)(2,1)} %param.16) | copy-start | bytes 1572868
  103.6 17.2 %copy-start.1 = (bf16[4,128,512]{2,1,0:T(8,128)(2,1)S(1)}, bf16[4,128,512]{2,1,0:T(8,128)(2,1)}, u32[]{:S(2)}) copy-start(bf16[4,128,512]{2,1,0:T(8,128)(2,1)} %param.11) | copy-start | bytes 1572868
  103.6 17.2 %copy-start.6 = (bf16[512,512]{1,0:T(8,128)(2,1)S(1)}, bf16[512,512]{1,0:T(8,128)(2,1)}, u32[]{:S(2)}) copy-start(bf16[512,512]{1,0:T(8,128)(2,1)} %param.17) | copy-start | bytes 1572868
  103.6 30.2 %copy-start.2 = (f32[512]{0:T(512)S(1)}, f32[512]{0:T(512)}, u32[]{:S(2)}) copy-start(f32[512]{0:T(512)} %param.19) | copy-start | bytes 6148
  103.6 30.2 %copy-start.3 = (f32[512]{0:T(512)S(1)}, f32[512]{0:T(512)}, u32[]{:S(2)}) copy-start(f32[512]{0:T(512)} %param.18) | copy-start | bytes 6148
  120.8 24.9 %slice-start = ((s8[4718592]{0:T(1024)(128)(4,1)}), s8[524288]{0:T(1024)(128)(4,1)S(1)}, s32[]{:S(2)}) async-start(s8[4718592]{0:T(1024)(128)(4,1)} %bitcast.74), calls=%async_computation.3 | async-start | bytes 1048576
  134.2 4.7 %collective-permute-start = (bf16[1,128,512]{2,1,0:T(8,128)(2,1)S(1)}, bf16[1,128,512]{2,1,0:T(8,128)(2,1)S(1)}, u32[]{:S(2)}, u32[]{:S(2)}) collective-permute-start(bf16[1,128,512]{2,1,0:T(8,128)(2,1)S(1)} %get-tuple-element.17), channel_id=1, source_target_pairs={{0,1},{1,2},{2,3},{3,4},{4,5},{5,6},{6,7},{7,8},{8,9},{9,10},{10,1... | collective-permute-start | bytes 393224 | tf_op jit(solution)/shard_map/ppermute | solution.py:38
  137.0 6.3 %collective-permute-start.1 = (bf16[1,128,512]{2,1,0:T(8,128)(2,1)S(1)}, bf16[1,128,512]{2,1,0:T(8,128)(2,1)S(1)}, u32[]{:S(2)}, u32[]{:S(2)}) collective-permute-start(bf16[1,128,512]{2,1,0:T(8,128)(2,1)S(1)} %get-tuple-element.18), channel_id=1, source_target_pairs={{1,0},{2,1},{3,2},{4,3},{5,4},{6,5},{7,6},{8,7},{9,8},{10,9},{11,1... | collective-permute-start | bytes 393224 | tf_op jit(solution)/shard_map/ppermute | solution.py:40
  143.5 2.3 %slice-start.1 = ((s8[4718592]{0:T(1024)(128)(4,1)}), s8[4194304]{0:T(1024)(128)(4,1)S(1)}, s32[]{:S(2)}) async-start(s8[4718592]{0:T(1024)(128)(4,1)} %bitcast.74), calls=%async_computation.4 | async-start | bytes 8388608
  146.3 2.7 %copy-start.4 = (f32[512]{0:T(512)S(1)}, f32[512]{0:T(512)}, u32[]{:S(2)}) copy-start(f32[512]{0:T(512)} %param.21) | copy-start | bytes 6148
Sparse Core Ops, SparseCore 0:
  27.7 52.6 all-gather.1
where the time goes:
time: 157 us
  waiting for transfers between devices  55.5 us (35%)
  matrix products  39.9 us (25%)
  blocking collectives  28.2 us (18%)
  other arithmetic  13.7 us (9%)
  between operations  13.6 us (9%)
  starting transfers between devices  4.64 us (3%)
    all_gather x1, waiting for transfers between devices, local(): piece = lax.all_gather(normed, 'row', axis=0, tiled=True)  51.1 us
    all_to_all x2, blocking collectives, copy_for_each(): return lax.all_to_all(copies, axis, split_axis=0, concat_axis=0, tiled=True)  28.2 us
    dot_general x1, matrix products, attend(): jnp.dot(expo.astype(jnp.bfloat16), value_piece, preferred_element_type=jn...  17.2 us
    dot_general x1, matrix products, attend(): jnp.einsum('qc,kc->qk', queries, key_piece, preferred_element_type=jnp.fl...  14.5 us
    reduce_sum x1, other arithmetic, attend(): denominator = jnp.sum(expo, axis=1)  8.68 us
    dot_general x9, matrix products, local(): jnp.dot(window, w_conv[row_tap, col_tap], preferred_element_type=jnp.floa...  6.07 us
    ppermute x1, waiting for transfers between devices, with_halo(): lax.ppermute(head, axis, [((i + 1) % count, i) for i in range(ends)])  4.35 us
  transfers between devices with their start and end apart: 3, of which 2 were waited for; matrix products, arithmetic and copies ran while one was open for 1% of the time, Pallas kernels for 0%

commit v1 on v0

--- a/solution.py
+++ b/solution.py
@@ -99,7 +99,9 @@
         jnp.zeros((count_rows,), jnp.float32),
         jnp.zeros((count_rows, C), jnp.float32),
     )
-    piece = lax.all_gather(normed, "row", axis=0, tiled=True)
+    piece = jnp.concatenate(
+        lax.all_to_all(jnp.stack([normed] * lax.axis_size("row")), "row", 0, 0), axis=0
+    )
     key_piece = jnp.dot(piece, w_key, preferred_element_type=jnp.float32).astype(jnp.bfloat16)
     value_piece = jnp.dot(piece, w_value, preferred_element_type=jnp.float32).astype(jnp.bfloat16)
     maxima, denominator, accumulated = attend(start_carry, key_piece, value_piece, queries)

time: 157 us -> 284 us (1.81)
  waiting for transfers between devices: 55.5 us -> 187 us
  between operations: 13.6 us -> 0.26 us
  starting transfers between devices: 4.64 us -> 9.9 us
  local copies, waits for them, and re-layouts: 1.52 us -> 5.56 us
    all_to_all x0 -> x1, waiting for transfers between devices: none -> 183 us  [local(): lax.all_to_all(jnp.stack([normed] * lax.axis_size('row')), 'row', 0, 0)]
    all_gather x1 -> x0, waiting for transfers between devices: 51.1 us -> none  [local(): piece = lax.all_gather(normed, 'row', axis=0, tiled=True)]
    all_to_all x0 -> x1, starting transfers between devices: none -> 5.26 us  [local(): lax.all_to_all(jnp.stack([normed] * lax.axis_size('row')), 'row', 0, 0)]
    another operation x0 -> x1, local copies, waits for them, and re-layouts: none -> 4.03 us  [local(): jnp.stack([normed] * lax.axis_size('row'))]
  transfers between devices with their start and end apart: 3 -> 3, of which waited for: 2 -> 2; matrix products, arithmetic and copies ran while one was open for 1% -> 0% of each run, Pallas kernels for 0% -> 0%
where the time goes in v1:
time: 284 us
  waiting for transfers between devices  187 us (66%)
  matrix products  38.7 us (14%)
  blocking collectives  29.3 us (10%)
  other arithmetic  12.9 us (5%)
  starting transfers between devices  9.9 us (3%)
  local copies, waits for them, and re-layouts  5.56 us (2%)
    all_to_all x1, waiting for transfers between devices, local(): lax.all_to_all(jnp.stack([normed] * lax.axis_size('row')), 'row', 0, 0)  183 us
    all_to_all x2, blocking collectives, copy_for_each(): return lax.all_to_all(copies, axis, split_axis=0, concat_axis=0, tiled=True)  29.3 us
    dot_general x1, matrix products, attend(): jnp.dot(expo.astype(jnp.bfloat16), value_piece, preferred_element_type=jn...  17.2 us
    dot_general x1, matrix products, attend(): jnp.einsum('qc,kc->qk', queries, key_piece, preferred_element_type=jnp.fl...  14.5 us
    reduce_sum x1, other arithmetic, attend(): denominator = jnp.sum(expo, axis=1)  8.68 us
    dot_general x9, matrix products, local(): jnp.dot(window, w_conv[row_tap, col_tap], preferred_element_type=jnp.floa...  6.07 us
  transfers between devices with their start and end apart: 3, of which 2 were waited for; matrix products, arithmetic and copies ran while one was open for 0% of the time, Pallas kernels for 0%

profile of v1, /device:TPU:1, one launch (start us, length us, event | category | flops | bytes accessed | tf_op | source)
XLA Modules:
  0.0 283.9 jit_solution(824836749497614837)
XLA Ops:
  0.0 1.3 convert_reduce_fusion.1
  1.3 0.1 reduce_sum.74
  1.4 0.1 reduce_sum.80
  1.4 0.1 reduce_sum.75
  1.6 0.1 reduce_sum.96
  1.7 0.1 pad_maximum_fusion.2
  1.8 16.8 %all_to_all.17 = f32[16,1,64]{2,1,0:T(1,128)S(1)} all-to-all(f32[16,1,64]{2,1,0:T(1,128)S(1)} %broadcast_in_dim.6), channel_id=1, replica_groups=mesh['img'=16,'row'=16] {'row'}, dimensions={0} | all-to-all | bytes 8192 | tf_op jit(solution)/shard_map/all_to_all | solution.py:14
  18.6 0.1 slice_multiply_fusion.1
  18.7 0.1 sub.42
  18.7 0.1 sub.43
  18.8 0.1 mul.72
  18.9 0.1 mul.73
  19.0 1.3 fusion.31
  20.2 4.0 %stack.2 = bf16[16,512,512]{2,1,0:T(8,128)(2,1)} broadcast(bf16[512,512]{1,0:T(8,128)(2,1)S(1)} %fusion.31), dimensions={1,2} | broadcast | bytes 8912896 | tf_op jit(solution)/shard_map/stack | solution.py:103
  24.3 5.3 %all-to-all-start.1 = ((bf16[16,512,512]{2,1,0:T(8,128)(2,1)}), bf16[16,512,512]{2,1,0:T(8,128)(2,1)}, u32[]{:S(2)}, u32[]{:S(2)}) async-start(bf16[16,512,512]{2,1,0:T(8,128)(2,1)} %stack.2), calls=%async_computation.1 | async-start | bytes 16777216 | tf_op jit(solution)/shard_map/all_to_all | solution.py:103
  29.5 0.4 convolution_convert_fusion.2
  30.0 183.0 %all-to-all-done.1 = bf16[16,512,512]{2,1,0:T(8,128)(2,1)} async-done(((bf16[16,512,512]{2,1,0:T(8,128)(2,1)}), bf16[16,512,512]{2,1,0:T(8,128)(2,1)}, u32[]{:S(2)}, u32[]{:S(2)}) %all-to-all-start.1) | async-done | bytes 8388640 | tf_op jit(solution)/shard_map/all_to_all | solution.py:103
  213.0 14.5 %multiply_reduce_fusion = (f32[512]{0:T(512)S(1)}, f32[512,8192]{1,0:T(8,128)}) fusion(bf16[512,512]{1,0:T(8,128)(2,1)S(1)} %convolution_convert_fusion.2, bf16[8192,512]{1,0:T(8,128)(2,1)} %bitcast.2, bf16[512,512]{1,0:T(8,128)(2,1)S(1)} %copy-done), kind=kOutput, calls=%fused_computation.1 | convolution fusion | flops 8602517504 | bytes 26216448 | tf_op jit(solution)/shard_map/qc,kc->qk/dot_general | solution.py:68
  227.5 8.7 %fusion = f32[512]{0:T(512)S(1)} fusion(f32[512,8192]{1,0:T(8,128)} %get-tuple-element.24, f32[512]{0:T(512)S(1)} %broadcast_maximum_fusion), kind=kLoop, calls=%fused_computation.2 | loop fusion | flops 12582400 | bytes 16781312 | tf_op jit(solution)/shard_map/reduce_sum | solution.py:72
  236.2 17.2 %fusion.15 = bf16[512,512]{1,0:T(8,128)(2,1)S(1)} fusion(bf16[8192,512]{1,0:T(8,128)(2,1)} %bitcast.2, bf16[512,512]{1,0:T(8,128)(2,1)S(1)} %copy-done.6, f32[512,8192]{1,0:T(8,128)} %get-tuple-element.24, f32[512]{0:T(512)S(1)} %broadcast_maximum_fusion, f32[512]{0:T(512)S(1)} %fusion), kind=kOutput, calls=%fused_computation.31 | convolution fusion | flops 8607236096 | bytes 26218496 | tf_op jit(solution)/shard_map/dot_general | solution.py:73
  253.5 0.5 convert_reduce_fusion
  254.0 0.1 reduce_sum.100
  254.0 0.3 reduce_sum.101
  254.3 0.1 reduce_sum.103
  254.4 0.1 reduce_sum.104
  254.5 0.1 pad_maximum_fusion.3
  254.6 12.4 %all_to_all.18 = f32[16,1,64]{2,1,0:T(1,128)S(1)} all-to-all(f32[16,1,64]{2,1,0:T(1,128)S(1)} %broadcast_in_dim.8), channel_id=1, replica_groups=mesh['img'=16,'row'=16] {'row'}, dimensions={0} | all-to-all | bytes 8192 | tf_op jit(solution)/shard_map/all_to_all | solution.py:14
  267.1 0.1 slice_multiply_fusion
  267.2 0.1 sub.50
  267.3 0.1 mul.82
  267.4 0.1 mul.83
  267.5 0.4 fusion.27
  267.9 2.7 collective-permute-start
  270.6 1.9 collective-permute-start.1
  272.5 4.3 %collective-permute-done.1 = bf16[1,128,512]{2,1,0:T(8,128)(2,1)S(1)} collective-permute-done((bf16[1,128,512]{2,1,0:T(8,128)(2,1)S(1)}, bf16[1,128,512]{2,1,0:T(8,128)(2,1)S(1)}, u32[]{:S(2)}, u32[]{:S(2)}) %collective-permute-start.1) | collective-permute-done | bytes 131104 | tf_op jit(solution)/shard_map/ppermute | solution.py:40
  276.9 0.2 fusion.36
  277.1 0.4 fusion.58
  277.5 1.7 fusion.46
  279.2 0.1 pad_maximum_fusion
  279.3 0.1 slice-done.1
  279.4 0.4 convolution_add_fusion.6
  279.9 0.4 convolution_add_fusion.5
  280.4 0.4 convolution_add_fusion.4
  280.8 0.4 convolution_add_fusion.3
  281.3 0.4 fusion.37
  281.7 0.4 convolution_add_fusion.2
  282.1 0.4 convolution_add_fusion.1
  282.6 1.3 fusion.10
  (28 shorter events, 0.2 us)
Async XLA Ops:
  0.0 213.0 %copy-start = (bf16[512,512]{1,0:T(8,128)(2,1)S(1)}, bf16[512,512]{1,0:T(8,128)(2,1)}, u32[]{:S(2)}) copy-start(bf16[512,512]{1,0:T(8,128)(2,1)} %param.15) | copy-start | bytes 1572868
  24.3 5.3 %copy-start.2 = (bf16[512,512]{1,0:T(8,128)(2,1)S(1)}, bf16[512,512]{1,0:T(8,128)(2,1)}, u32[]{:S(2)}) copy-start(bf16[512,512]{1,0:T(8,128)(2,1)} %param.14) | copy-start | bytes 1572868
  24.3 188.7 %all-to-all-start.1 = ((bf16[16,512,512]{2,1,0:T(8,128)(2,1)}), bf16[16,512,512]{2,1,0:T(8,128)(2,1)}, u32[]{:S(2)}, u32[]{:S(2)}) async-start(bf16[16,512,512]{2,1,0:T(8,128)(2,1)} %stack.2), calls=%async_computation.1 | async-start | bytes 16777216 | tf_op jit(solution)/shard_map/all_to_all | solution.py:103
  227.5 8.7 %copy-start.6 = (bf16[512,512]{1,0:T(8,128)(2,1)S(1)}, bf16[512,512]{1,0:T(8,128)(2,1)}, u32[]{:S(2)}) copy-start(bf16[512,512]{1,0:T(8,128)(2,1)} %param.16) | copy-start | bytes 1572868
  236.2 17.2 %copy-start.1 = (bf16[4,128,512]{2,1,0:T(8,128)(2,1)S(1)}, bf16[4,128,512]{2,1,0:T(8,128)(2,1)}, u32[]{:S(2)}) copy-start(bf16[4,128,512]{2,1,0:T(8,128)(2,1)} %param.11) | copy-start | bytes 1572868
  236.2 17.2 %copy-start.7 = (bf16[512,512]{1,0:T(8,128)(2,1)S(1)}, bf16[512,512]{1,0:T(8,128)(2,1)}, u32[]{:S(2)}) copy-start(bf16[512,512]{1,0:T(8,128)(2,1)} %param.17) | copy-start | bytes 1572868
  236.2 31.2 %copy-start.3 = (f32[512]{0:T(512)S(1)}, f32[512]{0:T(512)}, u32[]{:S(2)}) copy-start(f32[512]{0:T(512)} %param.19) | copy-start | bytes 6148
  236.2 31.2 %copy-start.4 = (f32[512]{0:T(512)S(1)}, f32[512]{0:T(512)}, u32[]{:S(2)}) copy-start(f32[512]{0:T(512)} %param.18) | copy-start | bytes 6148
  253.4 25.9 %slice-start = ((s8[4718592]{0:T(1024)(128)(4,1)}), s8[524288]{0:T(1024)(128)(4,1)S(1)}, s32[]{:S(2)}) async-start(s8[4718592]{0:T(1024)(128)(4,1)} %bitcast.75), calls=%async_computation.3 | async-start | bytes 1048576
  267.9 4.7 %collective-permute-start = (bf16[1,128,512]{2,1,0:T(8,128)(2,1)S(1)}, bf16[1,128,512]{2,1,0:T(8,128)(2,1)S(1)}, u32[]{:S(2)}, u32[]{:S(2)}) collective-permute-start(bf16[1,128,512]{2,1,0:T(8,128)(2,1)S(1)} %get-tuple-element.17), channel_id=1, source_target_pairs={{0,1},{1,2},{2,3},{3,4},{4,5},{5,6},{6,7},{7,8},{8,9},{9,10},{10,1... | collective-permute-start | bytes 393224 | tf_op jit(solution)/shard_map/ppermute | solution.py:38
  270.6 6.3 %collective-permute-start.1 = (bf16[1,128,512]{2,1,0:T(8,128)(2,1)S(1)}, bf16[1,128,512]{2,1,0:T(8,128)(2,1)S(1)}, u32[]{:S(2)}, u32[]{:S(2)}) collective-permute-start(bf16[1,128,512]{2,1,0:T(8,128)(2,1)S(1)} %get-tuple-element.18), channel_id=1, source_target_pairs={{1,0},{2,1},{3,2},{4,3},{5,4},{6,5},{7,6},{8,7},{9,8},{10,9},{11,1... | collective-permute-start | bytes 393224 | tf_op jit(solution)/shard_map/ppermute | solution.py:40
  277.1 2.3 slice-start.1
  279.9 2.7 copy-start.5
